TPU v7x, 256 devices: a whole 4x4x8 slice. The times are simulated.
256 devices in a mesh: edge: 64 (over y, z, x_lo), chan: 4 (over x_hi, core).
Axes of the slice: x: 4 (x_hi: 2, x_lo: 2; x = x_hi * 2 + x_lo), y: 4, z: 8, core: 2. Of those that a mesh axis runs over, the one named last changes fastest.
Arguments:
- node_states: bfloat16 [1024, 49, 256], P('edge', None, 'chan'), may hold values from -6 to 6
- edge_vectors: float32 [3, 32768], P(None, ('edge', 'chan')), may hold values from -5.6 to 5.6, as said below
- source_part: int32 [32768, 1], P('edge'), may hold values from 0 to 63; in each aligned block of 512 rows (0 to 511, 512 to 1023, ...) at most 16 rows name the same one
- source_slot: int32 [32768], P('edge'), may hold values from 0 to 15
- target_slot: int32 [32768], P('edge'), may hold values from 0 to 15
- live_edges: int32 [64], P('edge'), may hold values from 1 to 512, 24576 in all
- weight_zero: bfloat16 [7, 256, 7, 256], P(None, 'chan'), may hold values from -0.125 to 0.125
- weight_one: bfloat16 [2, 6, 256, 6, 256], P(None, None, 'chan'), may hold values from -0.109375 to 0.109375
- weight_two: bfloat16 [2, 5, 256, 5, 256], P(None, None, 'chan'), may hold values from -0.125 to 0.125
Outputs:
- aggregated: bfloat16 [1024, 49, 256], P('edge', None, 'chan')
Inputs may be any that keep to these rules, and one draw needn't show every extreme that they name: `source_part`: in each aligned block of 512 rows (the edges of one partition's slab) no partition number appears more than 16 times, and some number appears exactly 16 times. Edges are grouped by destination partition: the destination of an edge in slab p is node p * 16 + target_slot. `live_edges`: live slots stand at the front of each slab; the fullest slab is full. `edge_vectors`: every column has length between 0.8 and 5.6.
All inputs are finite; a program needn't handle non-finite values. No bound on the sum of `live_edges` on one device may be relied on, other than what follows from the above.
Results may differ from a plain program's by a relative error of at most 0.015.
Values may be sent and summed in bfloat16 or wider, within the bound.
A program may use at most 128 MiB of HBM per device.

v0:
```python
import math
import jax
import jax.numpy as jnp
import numpy as np
from jax import lax
from jax.sharding import PartitionSpec as P

LMAX = 6
MMAX = 2
cutoff_radius = 6.0
highest = lax.Precision.HIGHEST


def harmonics(coord_x, coord_y, coord_z, degree_top, order_top):
    results = {}
    real_part = [coord_x * 0.0 + 1.0]
    imag_part = [coord_x * 0.0]
    for azimuthal in range(1, order_top + 1):
        new_real = coord_x * real_part[-1] - coord_y * imag_part[-1]
        new_imag = coord_x * imag_part[-1] + coord_y * real_part[-1]
        real_part.append(new_real)
        imag_part.append(new_imag)
    for azimuthal in range(order_top + 1):
        start_value = (-1.0) ** azimuthal * math.prod(range(2 * azimuthal - 1, 0, -2))
        legendre = {azimuthal: coord_z * 0.0 + start_value}
        if azimuthal + 1 <= degree_top:
            legendre[azimuthal + 1] = coord_z * ((2 * azimuthal + 1) * start_value)
        for degree in range(azimuthal + 2, degree_top + 1):
            legendre[degree] = (
                (2 * degree - 1) * coord_z * legendre[degree - 1]
                - (degree + azimuthal - 1) * legendre[degree - 2]
            ) / (degree - azimuthal)
        for degree in range(azimuthal, degree_top + 1):
            factor = math.sqrt(
                (2 * degree + 1)
                / (4.0 * math.pi)
                * math.factorial(degree - azimuthal)
                / math.factorial(degree + azimuthal)
            )
            if azimuthal == 0:
                results[degree, 0] = factor * legendre[degree]
            else:
                results[degree, azimuthal] = (
                    math.sqrt(2.0) * factor * legendre[degree] * real_part[azimuthal]
                )
                results[degree, -azimuthal] = (
                    math.sqrt(2.0) * factor * legendre[degree] * imag_part[azimuthal]
                )
    return results


def kept_rows():
    row_list = [(degree, 0) for degree in range(LMAX + 1)]
    for azimuthal in range(1, MMAX + 1):
        row_list += [(degree, azimuthal) for degree in range(azimuthal, LMAX + 1)]
        row_list += [(degree, -azimuthal) for degree in range(azimuthal, LMAX + 1)]
    return row_list


def row_offsets():
    listing = []
    offset = 0
    for degree, azimuthal in kept_rows():
        listing.append((degree, offset))
        offset += 2 * degree + 1
    return listing


def invert_small(matrix):
    order_size = matrix.shape[0]
    work = np.concatenate([matrix, np.eye(order_size)], axis=1)
    for column in range(order_size):
        work[column] = work[column] / work[column, column]
        for row_index in range(order_size):
            if row_index != column:
                work[row_index] = work[row_index] - work[row_index, column] * work[column]
    return work[:, order_size:]


def sample_tables():
    sample_count = 2 * (LMAX + 1) ** 2
    positions = np.arange(sample_count) + 0.5
    height = 1.0 - 2.0 * positions / sample_count
    radius = np.sqrt(1.0 - height * height)
    azimuth = math.pi * (3.0 - math.sqrt(5.0)) * positions
    points = np.stack([radius * np.cos(azimuth), radius * np.sin(azimuth), height])
    values = harmonics(points[0], points[1], points[2], LMAX, LMAX)
    inverses = []
    for degree in range(LMAX + 1):
        sampled = np.stack([values[degree, azimuthal] for azimuthal in range(-degree, degree + 1)])
        inverses.append(sampled.T @ invert_small(sampled @ sampled.T))
    return (points, inverses)


def wigner_rows(vectors):
    length = jnp.sqrt(jnp.sum(vectors * vectors, axis=0))
    direction = vectors / length
    pick_first = jnp.where(jnp.abs(direction[0]) < 0.6, 1.0, 0.0).astype(jnp.float32)
    helper = jnp.stack([pick_first, 1.0 - pick_first, jnp.zeros_like(pick_first)])
    first_axis = jnp.cross(direction, helper, axis=0)
    first_axis = first_axis / jnp.sqrt(jnp.sum(first_axis * first_axis, axis=0))
    second_axis = jnp.cross(direction, first_axis, axis=0)
    frames = jnp.stack([first_axis, second_axis, direction])
    points, inverses = sample_tables()
    sample = jnp.asarray(points, jnp.float32)
    turned = jnp.einsum("rce,ck->rek", frames, sample, precision=highest)
    values = harmonics(turned[0], turned[1], turned[2], LMAX, MMAX)
    pieces = []
    for degree, azimuthal in kept_rows():
        table = jnp.asarray(inverses[degree], jnp.float32)
        pieces.append(jnp.dot(values[degree, azimuthal], table, precision=highest))
    compact = jnp.concatenate(pieces, axis=1)
    envelope = 0.5 * (jnp.cos(math.pi * length / cutoff_radius) + 1.0)
    return (compact, envelope)


def one_hot(indices, width):
    return (indices[:, None] == jnp.arange(width, dtype=jnp.int32)[None, :]).astype(jnp.bfloat16)


def rotate_forward(compact_t, scaling, sources):
    rows_out = []
    for degree, offset in row_offsets():
        span = 2 * degree + 1
        total = None
        for inner in range(span):
            term = compact_t[offset + inner].astype(jnp.float32)[None, :] * sources[
                degree * degree + inner
            ].astype(jnp.float32)
            total = term if total is None else total + term
        rows_out.append(total * scaling[None, :])
    return jnp.stack(rows_out, axis=0).astype(jnp.bfloat16)


def convolve(turned, weight_zero, weight_one, weight_two):
    end_zero = LMAX + 1
    end_one_plus = end_zero + LMAX
    end_one_minus = end_one_plus + LMAX
    end_two_plus = end_one_minus + LMAX - 1
    zero_part = turned[:end_zero]
    one_plus = turned[end_zero:end_one_plus]
    one_minus = turned[end_one_plus:end_one_minus]
    two_plus = turned[end_one_minus:end_two_plus]
    two_minus = turned[end_two_plus:]

    def contract(parts, weight, rows):
        left = jnp.concatenate(parts, axis=0)
        edges = left.shape[-1]
        left = left.reshape(-1, edges)
        right = weight.reshape(left.shape[0], -1)
        out = lax.dot_general(
            left, right, (((0,), (0,)), ((), ())), preferred_element_type=jnp.float32
        ).astype(jnp.bfloat16)
        return [out[:, row * 256 : (row + 1) * 256] for row in range(rows)]

    return (
        contract([zero_part], weight_zero, LMAX + 1)
        + contract([one_plus, -one_minus], weight_one, LMAX)
        + contract([one_minus, one_plus], weight_one, LMAX)
        + contract([two_plus, -two_minus], weight_two, LMAX - 1)
        + contract([two_minus, two_plus], weight_two, LMAX - 1)
    )


def shards(
    node_states,
    edge_vectors,
    source_part,
    source_slot,
    target_slot,
    live_edges,
    weight_zero,
    weight_one,
    weight_two,
):
    slab_size = source_slot.shape[0]
    local_nodes = node_states.shape[0]
    local_channels = node_states.shape[2]
    coef_count = node_states.shape[1]
    group_count = lax.axis_size("edge")
    node_flat = node_states.reshape(local_nodes, coef_count * local_channels)
    table = lax.all_gather(node_flat, "edge", axis=0, tiled=True)
    quarter, quarter_fade = wigner_rows(edge_vectors)
    packed = jnp.concatenate([quarter, quarter_fade[:, None]], axis=1).astype(jnp.bfloat16)
    packed_t = lax.all_gather(packed, "chan", axis=0, tiled=True).T
    compact_t, envelope = (packed_t[:-1], packed_t[-1])
    alive_mask = (jnp.arange(slab_size, dtype=jnp.int32) < live_edges[0]).astype(jnp.float32)
    scaling = envelope.astype(jnp.float32) * alive_mask
    source = source_part[:, 0] * local_nodes + source_slot
    select = one_hot(source, group_count * local_nodes)
    sources = (
        lax.dot_general(table, select, (((0,), (1,)), ((), ())), preferred_element_type=jnp.float32)
        .astype(jnp.bfloat16)
        .reshape(coef_count, local_channels, slab_size)
    )
    turned = rotate_forward(compact_t, scaling, sources)
    mixed = convolve(turned, weight_zero, weight_one, weight_two)
    selector = (jnp.arange(local_nodes, dtype=jnp.int32)[:, None] == target_slot[None, :]).astype(
        jnp.bfloat16
    )
    listing = row_offsets()
    sums = []
    for degree in range(LMAX + 1):
        span = 2 * degree + 1
        picked_rows = [
            (row, offset)
            for row, (row_degree, offset) in enumerate(listing)
            if row_degree == degree
        ]
        left = jnp.concatenate(
            [
                (compact_t[offset : offset + span][None] * selector[:, None]).reshape(
                    local_nodes * span, slab_size
                )
                for row, offset in picked_rows
            ],
            axis=1,
        )
        right = jnp.concatenate([mixed[row] for row, offset in picked_rows], axis=0)
        sums.append(
            jnp.dot(left, right, preferred_element_type=jnp.float32).reshape(local_nodes, span, -1)
        )
    partial = jnp.concatenate(sums, axis=1).astype(jnp.bfloat16)
    return lax.psum_scatter(partial, "chan", scatter_dimension=2, tiled=True)


def solution(mesh):
    in_specs = (
        P("edge", None, "chan"),
        P(None, ("edge", "chan")),
        P("edge", None),
        P("edge"),
        P("edge"),
        P("edge"),
        P(None, "chan", None, None),
        P(None, None, "chan", None, None),
        P(None, None, "chan", None, None),
    )
    out_specs = P("edge", None, "chan")
    return jax.shard_map(shards, mesh=mesh, in_specs=in_specs, out_specs=out_specs, check_vma=False)
```

profile of v0, /device:TPU:1, one launch (start us, length us, event | category | flops | bytes accessed | tf_op | source)
XLA Modules:
  0.0 408.8 jit_solution(11529215945910362788)
XLA Ops:
  6.5 1.0 copy.52
  11.4 1.0 fusion.442
  20.3 2.1 concatenate.68
  22.4 10.5 %all_gather.6 = bf16[512,236]{0,1:T(8,128)(2,1)S(1)} all-gather(bf16[128,236]{0,1:T(8,128)(2,1)S(1)} %concatenate.68), channel_id=1, replica_groups=mesh['edge'=64,'chan'=4] {'chan'}, dimensions={0}, use_global_device_ids=true | all-gather | bytes 302080 | tf_op jit(solution)/shard_map/all_gather | solution.py:185
  34.1 1.2 copy.55
  35.3 1.8 copy.63
  37.2 1.7 copy.54
  40.3 1.0 copy.53
  41.3 1.7 copy.61
  44.0 1.7 mul.5643
  45.7 1.7 mul.5646
  50.6 1.7 mul.5627
  52.3 1.7 mul.5630
  57.2 1.7 mul.5611
  58.9 1.7 mul.5614
  61.6 1.6 mul.5595
  63.2 1.6 mul.5598
  64.8 1.6 mul.5601
  67.3 1.6 mul.5199
  68.9 1.6 mul.5202
  70.5 1.6 mul.5205
  74.1 1.5 mul.4781
  75.6 1.5 mul.4784
  77.1 1.5 mul.4787
  79.3 1.3 add.1082
  85.1 1.7 constant_dynamic-update-slice_fusion.60
  86.8 1.5 constant_dynamic-update-slice_fusion.59
  90.4 1.0 constant_dynamic-update-slice_fusion.64
  104.1 173.3 %all-gather.2.cloned.1.call-done = bf16[1024,3136]{1,0:T(8,128)(2,1)} async-done(((bf16[16,3136]{1,0:T(8,128)(2,1)}), bf16[1024,3136]{1,0:T(8,128)(2,1)}) %all-gather.2.cloned.1.call-update) | async-done | bytes 6422544 | tf_op jit(solution)/shard_map/all_gather | solution.py:182
  277.4 8.6 %fusion = bf16[3136,512]{1,0:T(8,128)(2,1)S(1)} fusion(bf16[1024,3136]{1,0:T(8,128)(2,1)} %all-gather.2.cloned.1.call-done, s32[512]{0:T(512)} %add.1082), kind=kOutput, calls=%fused_computation.1 | convolution fusion | flops 3290464256 | bytes 9635840 | tf_op jit(solution)/shard_map/dot_general | solution.py:192
  293.0 1.1 convolution_convert_fusion.5
  300.0 1.4 convolution_convert_fusion.3
  301.7 1.4 convolution_convert_fusion.4
  304.2 1.0 copy-done.10
  305.2 1.2 convolution_convert_fusion.2
  306.4 1.2 convolution_convert_fusion.1
  309.4 1.1 copy-done.1
  310.6 1.1 copy-done.3
  312.5 2.0 convolution_convert_fusion.6
  315.2 1.0 convolution_convert_fusion.7
  316.3 1.0 reshape.3118
  317.3 1.5 convolution_convert_fusion.8
  318.9 1.5 convolution_convert_fusion.9
  322.8 1.0 copy.58
  323.8 2.1 reshape.3360
  325.8 73.7 %reduce-scatter.4.cloned.1.call-done = bf16[64,784]{1,0:T(8,128)(2,1)} async-done(((bf16[256,784]{1,0:T(8,128)(2,1)}), bf16[64,784]{1,0:T(8,128)(2,1)}) %reduce-scatter.4.cloned.1.call-update) | async-done | bytes 100368
  399.6 1.3 reshape.3361
  400.9 1.0 copy.57
  (656 shorter events, 61.3 us)
Async XLA Ops:
  6.5 6.0 %copy-start.34 = (f32[98,7]{1,0:T(8,128)S(1)}, f32[98,7]{1,0:T(8,128)}, u32[]{:S(2)}) copy-start(f32[98,7]{1,0:T(8,128)} %constant.140.clone) | copy-start | bytes 8236
  6.5 6.5 %copy-start.13 = (f32[98,5]{1,0:T(8,128)S(1)}, f32[98,5]{1,0:T(8,128)}, u32[]{:S(2)}) copy-start(f32[98,5]{1,0:T(8,128)} %constant.139.clone) | copy-start | bytes 5884
  6.5 7.5 %copy-start.29 = (f32[98,3]{1,0:T(8,128)S(1)}, f32[98,3]{1,0:T(8,128)}, u32[]{:S(2)}) copy-start(f32[98,3]{1,0:T(8,128)} %constant.138.clone) | copy-start | bytes 3532
  6.5 270.9 %all-gather.2.cloned.1.call-start = ((), (), s32[]{:S(2)}) async-start(), calls=%async_computation.1 | async-start | bytes 6656000 | tf_op jit(solution)/shard_map/all_gather | solution.py:182
  8.4 6.9 %copy-start.240 = (f32[98,13]{1,0:T(8,128)S(1)}, f32[98,13]{1,0:T(8,128)}, u32[]{:S(2)}) copy-start(f32[98,13]{1,0:T(8,128)} %constant.143.clone) | copy-start | bytes 15292
  8.4 391.1 %reduce-scatter.4.cloned.1.call-start = ((), (), s32[]{:S(2)}) async-start(), calls=%async_computation.2 | async-start | bytes 573440
  12.5 3.0 copy-start.239
  12.5 3.2 copy-start.238
  18.6 15.5 %copy-start.9 = (bf16[2,5,64,5,256]{4,2,3,1,0:T(8,128)(2,1)S(1)}, bf16[2,5,64,5,256]{4,2,3,1,0:T(8,128)(2,1)}, u32[]{:S(2)}) copy-start(bf16[2,5,64,5,256]{4,2,3,1,0:T(8,128)(2,1)} %param.49) | copy-start | bytes 4915204
  72.7 15.7 %copy-start.30 = (bf16[112,512]{1,0:T(8,128)(2,1)S(1)}, bf16[112,512]{1,0:T(8,128)(2,1)}, u32[]{:S(2)}) copy-start(bf16[112,512]{1,0:T(8,128)(2,1)} %mul.5601) | copy-start | bytes 344068
  73.4 17.0 %copy-start.27 = (bf16[144,512]{1,0:T(8,128)(2,1)S(1)}, bf16[144,512]{1,0:T(8,128)(2,1)}, u32[]{:S(2)}) copy-start(bf16[144,512]{1,0:T(8,128)(2,1)} %mul.5611) | copy-start | bytes 442372
  85.1 4.7 %copy-start.25 = (bf16[80,2560]{1,0:T(8,128)(2,1)}, bf16[80,2560]{1,0:T(8,128)(2,1)S(1)}, u32[]{:S(2)}) copy-start(bf16[80,2560]{1,0:T(8,128)(2,1)S(1)} %constant_dynamic-update-slice_fusion.31) | copy-start | bytes 1228804
  85.1 6.4 %copy-start.23 = (bf16[176,512]{1,0:T(8,128)(2,1)S(1)}, bf16[176,512]{1,0:T(8,128)(2,1)}, u32[]{:S(2)}) copy-start(bf16[176,512]{1,0:T(8,128)(2,1)} %mul.5627) | copy-start | bytes 540676
  88.4 3.2 copy-start.24
  89.0 2.5 copy-start.22
  91.5 4.5 %copy-start.14 = (bf16[144,2560]{1,0:T(8,128)(2,1)}, bf16[144,2560]{1,0:T(8,128)(2,1)S(1)}, u32[]{:S(2)}) copy-start(bf16[144,2560]{1,0:T(8,128)(2,1)S(1)} %constant_dynamic-update-slice_fusion.61) | copy-start | bytes 2211844
  91.5 2.3 copy-start.17
  91.5 3.0 copy-start.15
  91.6 3.7 copy-start.16
  104.0 182.1 %copy-start.185 = (f32[1,512]{1,0:T(1,128)S(1)}, f32[1,512]{1,0:T(1,128)}, u32[]{:S(2)}) copy-start(f32[1,512]{1,0:T(1,128)} %get-tuple-element.152) | copy-start | bytes 6148
  104.0 182.1 %copy-start.186 = (f32[1,512]{1,0:T(1,128)S(1)}, f32[1,512]{1,0:T(1,128)}, u32[]{:S(2)}) copy-start(f32[1,512]{1,0:T(1,128)} %get-tuple-element.153) | copy-start | bytes 6148
  104.0 182.1 %copy-start.187 = (f32[1,512]{1,0:T(1,128)S(1)}, f32[1,512]{1,0:T(1,128)}, u32[]{:S(2)}) copy-start(f32[1,512]{1,0:T(1,128)} %get-tuple-element.154) | copy-start | bytes 6148
  104.0 182.1 %copy-start.188 = (f32[1,512]{1,0:T(1,128)S(1)}, f32[1,512]{1,0:T(1,128)}, u32[]{:S(2)}) copy-start(f32[1,512]{1,0:T(1,128)} %get-tuple-element.155) | copy-start | bytes 6148
  104.0 182.1 %copy-start.189 = (f32[1,512]{1,0:T(1,128)S(1)}, f32[1,512]{1,0:T(1,128)}, u32[]{:S(2)}) copy-start(f32[1,512]{1,0:T(1,128)} %get-tuple-element.156) | copy-start | bytes 6148
  104.0 182.4 %copy-start.162 = (f32[1,512]{1,0:T(1,128)S(1)}, f32[1,512]{1,0:T(1,128)}, u32[]{:S(2)}) copy-start(f32[1,512]{1,0:T(1,128)} %get-tuple-element.148) | copy-start | bytes 6148
  104.1 182.4 %copy-start.163 = (f32[1,512]{1,0:T(1,128)S(1)}, f32[1,512]{1,0:T(1,128)}, u32[]{:S(2)}) copy-start(f32[1,512]{1,0:T(1,128)} %get-tuple-element.149) | copy-start | bytes 6148
  104.1 182.4 %copy-start.164 = (f32[1,512]{1,0:T(1,128)S(1)}, f32[1,512]{1,0:T(1,128)}, u32[]{:S(2)}) copy-start(f32[1,512]{1,0:T(1,128)} %get-tuple-element.150) | copy-start | bytes 6148
  104.1 182.4 %copy-start.165 = (f32[1,512]{1,0:T(1,128)S(1)}, f32[1,512]{1,0:T(1,128)}, u32[]{:S(2)}) copy-start(f32[1,512]{1,0:T(1,128)} %get-tuple-element.151) | copy-start | bytes 6148
  277.4 9.1 %copy-start.197 = (f32[1,512]{1,0:T(1,128)S(1)}, f32[1,512]{1,0:T(1,128)}, u32[]{:S(2)}) copy-start(f32[1,512]{1,0:T(1,128)} %get-tuple-element.144) | copy-start | bytes 6148
  277.4 9.1 %copy-start.198 = (f32[1,512]{1,0:T(1,128)S(1)}, f32[1,512]{1,0:T(1,128)}, u32[]{:S(2)}) copy-start(f32[1,512]{1,0:T(1,128)} %get-tuple-element.145) | copy-start | bytes 6148
  277.4 9.1 %copy-start.199 = (f32[1,512]{1,0:T(1,128)S(1)}, f32[1,512]{1,0:T(1,128)}, u32[]{:S(2)}) copy-start(f32[1,512]{1,0:T(1,128)} %get-tuple-element.146) | copy-start | bytes 6148
  288.1 2.3 copy-start.46
  288.1 2.3 copy-start.47
  288.3 2.3 copy-start.39
  288.3 2.3 copy-start.40
  288.3 2.3 copy-start.41
  288.4 2.3 copy-start.42
  288.4 2.3 copy-start.43
  288.4 2.3 copy-start.38
  289.2 2.4 copy-start.211
  289.3 2.4 copy-start.212
  289.3 2.4 copy-start.213
  289.3 2.4 copy-start.214
  289.3 2.4 copy-start.215
  289.3 2.4 copy-start.216
  289.3 2.4 copy-start.217
  312.5 2.8 copy-start.2
  316.3 2.6 copy-start.8
  (195 other events, 297.2 us)
Sparse Core Ops, SparseCore 0:
  9.1 268.2 all-gather.1
  326.0 73.5 reduce-scatter.3
where the time goes:
time: 410 us; the launch traced here: 409 us
  waiting for transfers between devices  247 us (60%)
  local copies, waits for them, and re-layouts  75.8 us (18%)
  matrix products  30.5 us (7%)
  other arithmetic  26.9 us (7%)
  between operations  18.1 us (4%)
  blocking collectives  10.5 us (3%)
    all_gather x1, waiting for transfers between devices, shards(): table = lax.all_gather(node_flat, 'edge', axis=0, tiled=True)  173 us
    unnamed x3, waiting for transfers between devices  73.7 us
    unnamed x534, local copies, waits for them, and re-layouts  36.1 us
    mul x28, local copies, waits for them, and re-layouts, shards(): compact_t[offset:offset + span][None] * selector[:, None]  30.4 us
    all_gather x1, blocking collectives, shards(): packed_t = lax.all_gather(packed, 'chan', axis=0, tiled=True).T  10.5 us
    mul x14, other arithmetic, rotate_forward(): compact_t[offset + inner].astype(jnp.float32)[None, :]  9.2 us
    dot_general x1, matrix products, shards(): lax.dot_general(table, select, (((0,), (1,)), ((), ())), preferred_elemen...  8.62 us
  transfers between devices with their start and end apart: 2, of which 2 were waited for; matrix products, arithmetic and copies ran while one was open for 20% of the time, Pallas kernels for 0%

commit v1 on v0

--- a/solution.py
+++ b/solution.py
@@ -179,7 +179,9 @@
     coef_count = node_states.shape[1]
     group_count = lax.axis_size("edge")
     node_flat = node_states.reshape(local_nodes, coef_count * local_channels)
-    table = lax.all_gather(node_flat, "edge", axis=0, tiled=True)
+    table = jnp.concatenate(
+        lax.all_to_all(jnp.stack([node_flat] * lax.axis_size("edge")), "edge", 0, 0), axis=0
+    )
     quarter, quarter_fade = wigner_rows(edge_vectors)
     packed = jnp.concatenate([quarter, quarter_fade[:, None]], axis=1).astype(jnp.bfloat16)
     packed_t = lax.all_gather(packed, "chan", axis=0, tiled=True).T

time: 410 us -> 262 us (0.64)
  waiting for transfers between devices: 247 us -> 87.2 us
  starting transfers between devices: 0.04 us -> 14 us
    all_gather x1 -> x0, waiting for transfers between devices: 173 us -> none  [shards(): table = lax.all_gather(node_flat, 'edge', axis=0, tiled=True)]
    all_to_all x0 -> x1, waiting for transfers between devices: none -> 53.7 us  [shards(): lax.all_to_all(jnp.stack([node_flat] * lax.axis_size('edge')), 'edge', 0, 0)]
    unnamed x3 -> x2, waiting for transfers between devices: 73.7 us -> 33.5 us
    all_to_all x0 -> x1, starting transfers between devices: none -> 13.9 us  [shards(): lax.all_to_all(jnp.stack([node_flat] * lax.axis_size('edge')), 'edge', 0, 0)]
    unnamed x534 -> x538, local copies, waits for them, and re-layouts: 36.1 us -> 36.1 us
  transfers between devices with their start and end apart: 2 -> 2, of which waited for: 2 -> 2; matrix products, arithmetic and copies ran while one was open for 20% -> 30% of each run, Pallas kernels for 0% -> 0%
where the time goes in v1:
time: 262 us; the launch traced here: 260 us
  waiting for transfers between devices  87.2 us (33%)
  local copies, waits for them, and re-layouts  78.4 us (30%)
  matrix products  29.8 us (11%)
  other arithmetic  24.1 us (9%)
  between operations  18.1 us (7%)
  starting transfers between devices  14 us (5%)
  blocking collectives  8.55 us (3%)
    all_to_all x1, waiting for transfers between devices, shards(): lax.all_to_all(jnp.stack([node_flat] * lax.axis_size('edge')), 'edge', 0, 0)  53.7 us
    unnamed x538, local copies, waits for them, and re-layouts  36.1 us
    unnamed x2, waiting for transfers between devices  33.5 us
    mul x28, local copies, waits for them, and re-layouts, shards(): compact_t[offset:offset + span][None] * selector[:, None]  30.5 us
    all_to_all x1, starting transfers between devices, shards(): lax.all_to_all(jnp.stack([node_flat] * lax.axis_size('edge')), 'edge', 0, 0)  13.9 us
    mul x14, other arithmetic, rotate_forward(): compact_t[offset + inner].astype(jnp.float32)[None, :]  9.25 us
    dot_general x1, matrix products, shards(): lax.dot_general(table, select, (((0,), (1,)), ((), ())), preferred_elemen...  8.64 us
    all_gather x1, blocking collectives, shards(): packed_t = lax.all_gather(packed, 'chan', axis=0, tiled=True).T  8.55 us
  transfers between devices with their start and end apart: 2, of which 2 were waited for; matrix products, arithmetic and copies ran while one was open for 30% of the time, Pallas kernels for 0%

profile of v1, /device:TPU:1, one launch (start us, length us, event | category | flops | bytes accessed | tf_op | source)
XLA Modules:
  0.0 260.1 jit_solution(2935120403479059129)
XLA Ops:
  6.5 1.0 copy.52
  7.7 3.2 %stack.24 = bf16[64,16,3136]{2,1,0:T(8,128)(2,1)} broadcast(bf16[16,3136]{1,0:T(8,128)(2,1)S(1)} %stack_reshape.2), dimensions={1,2} | broadcast | bytes 6522880 | tf_op jit(solution)/shard_map/stack | solution.py:183
  10.9 13.9 %all-to-all-start = ((bf16[64,16,3136]{2,1,0:T(8,128)(2,1)}), bf16[64,16,3136]{2,1,0:T(8,128)(2,1)}, u32[]{:S(2)}, u32[]{:S(2)}) async-start(bf16[64,16,3136]{2,1,0:T(8,128)(2,1)} %stack.24), calls=%async_computation | async-start | bytes 13107200 | tf_op jit(solution)/shard_map/all_to_all | solution.py:183
  33.4 2.1 concatenate.68
  35.5 8.5 %all_gather.3 = bf16[512,236]{0,1:T(8,128)(2,1)S(1)} all-gather(bf16[128,236]{0,1:T(8,128)(2,1)S(1)} %concatenate.68), channel_id=1, replica_groups=mesh['edge'=64,'chan'=4] {'chan'}, dimensions={0}, use_global_device_ids=true | all-gather | bytes 302080 | tf_op jit(solution)/shard_map/all_gather | solution.py:187
  45.2 1.2 copy.55
  46.4 1.8 copy.63
  48.4 1.7 copy.54
  51.5 1.0 copy.53
  52.5 1.7 copy.61
  55.1 1.7 mul.5643
  56.8 1.7 mul.5646
  61.8 1.7 mul.5627
  63.5 1.7 mul.5630
  68.4 1.7 mul.5611
  70.1 1.7 mul.5614
  72.8 1.6 mul.5595
  74.4 1.6 mul.5598
  76.0 1.6 mul.5601
  78.5 1.6 mul.5199
  80.0 1.6 mul.5202
  81.6 1.6 mul.5205
  85.3 1.5 mul.4781
  86.8 1.5 mul.4784
  88.3 1.5 mul.4787
  90.5 1.2 add.1082
  96.2 1.8 constant_dynamic-update-slice_fusion.60
  97.9 1.6 constant_dynamic-update-slice_fusion.59
  115.1 53.7 %all-to-all-done = bf16[64,16,3136]{2,1,0:T(8,128)(2,1)} async-done(((bf16[64,16,3136]{2,1,0:T(8,128)(2,1)}), bf16[64,16,3136]{2,1,0:T(8,128)(2,1)}, u32[]{:S(2)}, u32[]{:S(2)}) %all-to-all-start) | async-done | bytes 6422560 | tf_op jit(solution)/shard_map/all_to_all | solution.py:183
  169.0 8.6 %fusion = bf16[3136,512]{1,0:T(8,128)(2,1)S(1)} fusion(bf16[1024,3136]{1,0:T(8,128)(2,1)} %bitcast.23, s32[512]{0:T(512)} %add.1082), kind=kOutput, calls=%fused_computation.1 | convolution fusion | flops 3290464256 | bytes 9635840 | tf_op jit(solution)/shard_map/dot_general | solution.py:194
  184.6 1.1 convolution_convert_fusion.5
  191.6 1.4 convolution_convert_fusion.3
  193.3 1.4 convolution_convert_fusion.4
  195.7 1.0 copy-done.10
  196.7 1.2 convolution_convert_fusion.2
  197.9 1.2 convolution_convert_fusion.1
  201.0 1.1 copy-done.1
  202.1 1.1 copy-done.3
  204.0 2.0 convolution_convert_fusion.6
  206.8 1.0 convolution_convert_fusion.7
  207.8 1.0 reshape.3120
  208.9 1.5 convolution_convert_fusion.8
  210.4 1.5 convolution_convert_fusion.9
  214.3 1.0 copy.58
  215.3 2.1 reshape.3362
  217.4 33.4 %reduce-scatter.4.cloned.1.call-done = bf16[64,784]{1,0:T(8,128)(2,1)} async-done(((bf16[256,784]{1,0:T(8,128)(2,1)}), bf16[64,784]{1,0:T(8,128)(2,1)}) %reduce-scatter.4.cloned.1.call-update) | async-done | bytes 100368
  250.9 1.3 reshape.3363
  252.2 1.0 copy.57
  (660 shorter events, 59.2 us)
Async XLA Ops:
  10.9 14.0 %copy-start.38 = (f32[3,128]{1,0:T(4,128)S(1)}, f32[3,128]{1,0:T(4,128)}, u32[]{:S(2)}) copy-start(f32[3,128]{1,0:T(4,128)} %param.42) | copy-start | bytes 4612
  10.9 14.3 %copy-start.237 = (f32[3,98,1]{1,0,2:T(4,128)S(1)}, f32[3,98,1]{1,0,2:T(4,128)}, u32[]{:S(2)}) copy-start(f32[3,98,1]{1,0,2:T(4,128)} %constant.147) | copy-start | bytes 3532
  10.9 14.7 %copy-start.34 = (f32[98,7]{1,0:T(8,128)S(1)}, f32[98,7]{1,0:T(8,128)}, u32[]{:S(2)}) copy-start(f32[98,7]{1,0:T(8,128)} %constant.140.clone) | copy-start | bytes 8236
  10.9 15.2 %copy-start.13 = (f32[98,5]{1,0:T(8,128)S(1)}, f32[98,5]{1,0:T(8,128)}, u32[]{:S(2)}) copy-start(f32[98,5]{1,0:T(8,128)} %constant.139.clone) | copy-start | bytes 5884
  10.9 158.0 %all-to-all-start = ((bf16[64,16,3136]{2,1,0:T(8,128)(2,1)}), bf16[64,16,3136]{2,1,0:T(8,128)(2,1)}, u32[]{:S(2)}, u32[]{:S(2)}) async-start(bf16[64,16,3136]{2,1,0:T(8,128)(2,1)} %stack.24), calls=%async_computation | async-start | bytes 13107200 | tf_op jit(solution)/shard_map/all_to_all | solution.py:183
  24.8 2.3 copy-start.29
  24.8 3.5 %copy-start.242 = (f32[98,13]{1,0:T(8,128)S(1)}, f32[98,13]{1,0:T(8,128)}, u32[]{:S(2)}) copy-start(f32[98,13]{1,0:T(8,128)} %constant.143.clone) | copy-start | bytes 15292
  24.9 226.0 %reduce-scatter.4.cloned.1.call-start = ((), (), s32[]{:S(2)}) async-start(), calls=%async_computation.2 | async-start | bytes 573440
  25.6 3.0 %copy-start.241 = (f32[98,11]{1,0:T(8,128)S(1)}, f32[98,11]{1,0:T(8,128)}, u32[]{:S(2)}) copy-start(f32[98,11]{1,0:T(8,128)} %constant.142.clone) | copy-start | bytes 12940
  25.6 3.2 %copy-start.240 = (f32[98,9]{1,0:T(8,128)S(1)}, f32[98,9]{1,0:T(8,128)}, u32[]{:S(2)}) copy-start(f32[98,9]{1,0:T(8,128)} %constant.141.clone) | copy-start | bytes 10588
  31.6 13.6 %copy-start.9 = (bf16[2,5,64,5,256]{4,2,3,1,0:T(8,128)(2,1)S(1)}, bf16[2,5,64,5,256]{4,2,3,1,0:T(8,128)(2,1)}, u32[]{:S(2)}) copy-start(bf16[2,5,64,5,256]{4,2,3,1,0:T(8,128)(2,1)} %param.49) | copy-start | bytes 4915204
  83.9 15.6 %copy-start.30 = (bf16[112,512]{1,0:T(8,128)(2,1)S(1)}, bf16[112,512]{1,0:T(8,128)(2,1)}, u32[]{:S(2)}) copy-start(bf16[112,512]{1,0:T(8,128)(2,1)} %mul.5601) | copy-start | bytes 344068
  84.5 16.9 %copy-start.27 = (bf16[144,512]{1,0:T(8,128)(2,1)S(1)}, bf16[144,512]{1,0:T(8,128)(2,1)}, u32[]{:S(2)}) copy-start(bf16[144,512]{1,0:T(8,128)(2,1)} %mul.5611) | copy-start | bytes 442372
  96.2 4.7 %copy-start.25 = (bf16[80,2560]{1,0:T(8,128)(2,1)}, bf16[80,2560]{1,0:T(8,128)(2,1)S(1)}, u32[]{:S(2)}) copy-start(bf16[80,2560]{1,0:T(8,128)(2,1)S(1)} %constant_dynamic-update-slice_fusion.31) | copy-start | bytes 1228804
  96.2 6.4 %copy-start.23 = (bf16[176,512]{1,0:T(8,128)(2,1)S(1)}, bf16[176,512]{1,0:T(8,128)(2,1)}, u32[]{:S(2)}) copy-start(bf16[176,512]{1,0:T(8,128)(2,1)} %mul.5627) | copy-start | bytes 540676
  99.5 3.1 %copy-start.24 = (bf16[176,512]{1,0:T(8,128)(2,1)S(1)}, bf16[176,512]{1,0:T(8,128)(2,1)}, u32[]{:S(2)}) copy-start(bf16[176,512]{1,0:T(8,128)(2,1)} %mul.5630) | copy-start | bytes 540676
  100.1 2.5 copy-start.22
  102.6 4.5 %copy-start.14 = (bf16[144,2560]{1,0:T(8,128)(2,1)}, bf16[144,2560]{1,0:T(8,128)(2,1)S(1)}, u32[]{:S(2)}) copy-start(bf16[144,2560]{1,0:T(8,128)(2,1)S(1)} %constant_dynamic-update-slice_fusion.61) | copy-start | bytes 2211844
  102.6 2.3 copy-start.17
  102.6 3.0 %copy-start.15 = (bf16[208,512]{1,0:T(8,128)(2,1)S(1)}, bf16[208,512]{1,0:T(8,128)(2,1)}, u32[]{:S(2)}) copy-start(bf16[208,512]{1,0:T(8,128)(2,1)} %mul.5652) | copy-start | bytes 638980
  102.7 3.7 %copy-start.16 = (bf16[208,512]{1,0:T(8,128)(2,1)S(1)}, bf16[208,512]{1,0:T(8,128)(2,1)}, u32[]{:S(2)}) copy-start(bf16[208,512]{1,0:T(8,128)(2,1)} %mul.5655) | copy-start | bytes 638980
  168.9 8.8 %copy-start.186 = (f32[1,512]{1,0:T(1,128)S(1)}, f32[1,512]{1,0:T(1,128)}, u32[]{:S(2)}) copy-start(f32[1,512]{1,0:T(1,128)} %get-tuple-element.152) | copy-start | bytes 6148
  168.9 8.8 %copy-start.187 = (f32[1,512]{1,0:T(1,128)S(1)}, f32[1,512]{1,0:T(1,128)}, u32[]{:S(2)}) copy-start(f32[1,512]{1,0:T(1,128)} %get-tuple-element.153) | copy-start | bytes 6148
  168.9 8.8 %copy-start.188 = (f32[1,512]{1,0:T(1,128)S(1)}, f32[1,512]{1,0:T(1,128)}, u32[]{:S(2)}) copy-start(f32[1,512]{1,0:T(1,128)} %get-tuple-element.154) | copy-start | bytes 6148
  168.9 8.8 %copy-start.189 = (f32[1,512]{1,0:T(1,128)S(1)}, f32[1,512]{1,0:T(1,128)}, u32[]{:S(2)}) copy-start(f32[1,512]{1,0:T(1,128)} %get-tuple-element.155) | copy-start | bytes 6148
  168.9 8.8 %copy-start.190 = (f32[1,512]{1,0:T(1,128)S(1)}, f32[1,512]{1,0:T(1,128)}, u32[]{:S(2)}) copy-start(f32[1,512]{1,0:T(1,128)} %get-tuple-element.156) | copy-start | bytes 6148
  168.9 9.2 %copy-start.163 = (f32[1,512]{1,0:T(1,128)S(1)}, f32[1,512]{1,0:T(1,128)}, u32[]{:S(2)}) copy-start(f32[1,512]{1,0:T(1,128)} %get-tuple-element.148) | copy-start | bytes 6148
  168.9 9.2 %copy-start.164 = (f32[1,512]{1,0:T(1,128)S(1)}, f32[1,512]{1,0:T(1,128)}, u32[]{:S(2)}) copy-start(f32[1,512]{1,0:T(1,128)} %get-tuple-element.149) | copy-start | bytes 6148
  168.9 9.2 %copy-start.165 = (f32[1,512]{1,0:T(1,128)S(1)}, f32[1,512]{1,0:T(1,128)}, u32[]{:S(2)}) copy-start(f32[1,512]{1,0:T(1,128)} %get-tuple-element.150) | copy-start | bytes 6148
  168.9 9.2 %copy-start.166 = (f32[1,512]{1,0:T(1,128)S(1)}, f32[1,512]{1,0:T(1,128)}, u32[]{:S(2)}) copy-start(f32[1,512]{1,0:T(1,128)} %get-tuple-element.151) | copy-start | bytes 6148
  168.9 9.2 %copy-start.198 = (f32[1,512]{1,0:T(1,128)S(1)}, f32[1,512]{1,0:T(1,128)}, u32[]{:S(2)}) copy-start(f32[1,512]{1,0:T(1,128)} %get-tuple-element.144) | copy-start | bytes 6148
  168.9 9.2 %copy-start.199 = (f32[1,512]{1,0:T(1,128)S(1)}, f32[1,512]{1,0:T(1,128)}, u32[]{:S(2)}) copy-start(f32[1,512]{1,0:T(1,128)} %get-tuple-element.145) | copy-start | bytes 6148
  168.9 9.2 %copy-start.200 = (f32[1,512]{1,0:T(1,128)S(1)}, f32[1,512]{1,0:T(1,128)}, u32[]{:S(2)}) copy-start(f32[1,512]{1,0:T(1,128)} %get-tuple-element.146) | copy-start | bytes 6148
  179.9 2.3 copy-start.40
  179.9 2.3 copy-start.41
  179.9 2.3 copy-start.42
  179.9 2.3 copy-start.43
  179.9 2.3 copy-start.44
  180.0 2.4 copy-start.39
  180.8 2.4 copy-start.212
  180.8 2.4 copy-start.213
  180.8 2.4 copy-start.214
  180.8 2.4 copy-start.215
  180.8 2.4 copy-start.216
  180.9 2.4 copy-start.217
  180.9 2.4 copy-start.218
  204.0 2.8 %copy-start.2 = (bf16[2560,256]{1,0:T(8,128)(2,1)S(1)}, bf16[2560,256]{1,0:T(8,128)(2,1)}, u32[]{:S(2)}) copy-start(bf16[2560,256]{1,0:T(8,128)(2,1)} %copy-done.1) | copy-start | bytes 3932164
  207.8 2.6 %copy-start.8 = (bf16[2560,256]{1,0:T(8,128)(2,1)S(1)}, bf16[2560,256]{1,0:T(8,128)(2,1)}, u32[]{:S(2)}) copy-start(bf16[2560,256]{1,0:T(8,128)(2,1)} %copy-done.7) | copy-start | bytes 3932164
  (197 other events, 301.0 us)
Sparse Core Ops, SparseCore 0:
  217.5 33.2 reduce-scatter.3
